TPU v7x, 32 devices: a whole 2x2x4 slice. The times are simulated.
32 devices in a mesh: replica: 2 (over x), tp: 8 (over z, y), sub: 2 (over core).
Axes of the slice: x: 2, y: 2, z: 4, core: 2. Of those that a mesh axis runs over, the one named last changes fastest.
Arguments:
- hidden_in: bfloat16 [8, 8192], P('replica'), parts along dimension 0, may hold values from -6 to 6
- norm_gain: float32 [16384], P('replica'), parts along dimension 0, may hold values from 0.1 to 1.9
- wqkv_old: bfloat16 [16, 2, 1280, 4096], P(('replica', 'tp'), 'sub'), parts along dimension 0, may hold values from -0.1875 to 0.1875
- wo: bfloat16 [16384, 8192], P(('replica', 'tp', 'sub')), parts along dimension 0, may hold values from -0.0625 to 0.0625
- key_cache: bfloat16 [8, 4096, 1024], P('replica', ('tp', 'sub')), parts along dimension 0, may hold values from -240 to 240
- value_cache: bfloat16 [8, 4096, 1024], P('replica', ('tp', 'sub')), parts along dimension 0, may hold values from -6 to 6
- lengths: int32 [8], P('replica'), parts along dimension 0, may hold values from 1 to 4096
- section_order: int32 [32], P('replica'), parts along dimension 0, may hold values from 0 to 15, each once
Outputs:
- mixed_out: bfloat16 [8, 8192], P('replica'), parts along dimension 0
- wqkv_new: bfloat16 [16, 2, 640, 8192], P(('replica', 'tp'), 'sub'), parts along dimension 0
There are 2 independent parts, one for each index of `replica`. A program takes and returns all parts, laid end to end along the dimension named above; each array names one. Nothing has to cross between parts.
Inputs may be any that keep to these rules, and one draw needn't show every extreme that they name: `section_order`: each input row block appears once. The new token's position is lengths[b].
All inputs are finite; a program needn't handle non-finite values.
Results may differ from a plain program's by a relative error of at most 0.0085.
The roundings to bfloat16 on the way count: a program that leaves them out, or rounds other values in their place, can miss the bound.
Values may be sent and summed in bfloat16 or wider, within the bound.
A program may use at most 128 MiB of HBM per device.

v0:
```python
import math

import jax
import jax.numpy as jnp
from jax import lax
from jax.sharding import PartitionSpec as P

HEADS = 64
KV_HEADS = 8
HEAD_DIM = 128
RANKS = 8
ROW_BLOCKS = 16


def passed_along(value, axis, steps):
    count = lax.axis_size(axis)
    pairs = [(source, (source + steps) % count) for source in range(count)]
    return lax.ppermute(value, axis, pairs)


def rotary(values, positions):
    half = values.shape[-1] // 2
    freqs = 500000.0 ** (-jnp.arange(half, dtype=jnp.float32) * 2.0 / values.shape[-1])
    angles = positions.astype(jnp.float32)[:, None] * freqs[None, :]
    cosine = jnp.cos(angles)[:, None, :]
    sine = jnp.sin(angles)[:, None, :]
    first_half = values[..., :half]
    second_half = values[..., half:]
    return jnp.concatenate(
        [first_half * cosine - second_half * sine, second_half * cosine + first_half * sine], -1
    )


def rms_normed(hidden_in, norm_gain):
    widened = hidden_in.astype(jnp.float32)
    factor = lax.rsqrt(jnp.mean(widened * widened, -1, keepdims=True) + 1e-05)
    return (widened, (widened * factor * norm_gain).astype(jnp.bfloat16))


def shards(hidden_in, norm_gain, wqkv_old, wo, key_cache, value_cache, lengths, section_order):
    tp_count = lax.axis_size("tp")
    section_count = tp_count // 4
    per_section = ROW_BLOCKS // section_count
    tp_index = lax.axis_index("tp")
    sub_index = lax.axis_index("sub")
    own_section = tp_index // 4
    device_rank = tp_index * 2 + sub_index
    cols_dev = wqkv_old.shape[2] // section_count
    rows_old = wqkv_old.shape[3]
    block_rows = rows_old // per_section
    old_block = wqkv_old[0, 0].reshape(section_count, cols_dev, rows_old)
    slot_ids = jnp.arange(section_count, dtype=jnp.int32)
    arrived = [lax.dynamic_index_in_dim(old_block, own_section, 0, keepdims=False)]
    for offset in range(1, section_count):
        outgoing = lax.dynamic_index_in_dim(
            old_block, (own_section + offset) % section_count, 0, keepdims=False
        )
        arrived.append(passed_along(outgoing, "tp", 4 * offset))
    received = jnp.stack(arrived, 0)
    sources = (own_section - slot_ids) % section_count
    block_ids = jnp.arange(ROW_BLOCKS, dtype=jnp.int32)
    local_source = (
        sources[:, None] * per_section + jnp.arange(per_section, dtype=jnp.int32)[None, :]
    ).reshape(ROW_BLOCKS)
    target_block = jnp.take(section_order, local_source, axis=0)
    placing = (target_block[None, :] == block_ids[:, None]).astype(jnp.bfloat16)
    received_blocks = jnp.transpose(
        received.reshape(section_count, cols_dev, per_section, block_rows), (0, 2, 1, 3)
    ).reshape(ROW_BLOCKS, cols_dev, block_rows)
    new_weight = jnp.einsum(
        "sa,acr->csr", placing, received_blocks, preferred_element_type=jnp.float32
    ).astype(jnp.bfloat16)
    new_weight = new_weight.reshape(cols_dev, ROW_BLOCKS * block_rows)
    widened, normed = rms_normed(hidden_in, norm_gain)
    projected = lax.dot_general(
        normed, new_weight, (((1,), (1,)), ((), ())), preferred_element_type=jnp.float32
    ).astype(jnp.bfloat16)
    gathered = lax.all_gather(projected[:, None, :], ("tp", "sub"), axis=1, tiled=True)
    seq_count = hidden_in.shape[0]
    projected_all = jnp.transpose(
        gathered.reshape(seq_count, section_count, RANKS, cols_dev), (0, 2, 1, 3)
    ).reshape(seq_count, -1)
    q_width = HEADS * HEAD_DIM
    kv_width = KV_HEADS * HEAD_DIM
    groups = HEADS // KV_HEADS
    queries = rotary(
        projected_all[:, :q_width].astype(jnp.float32).reshape(seq_count, HEADS, HEAD_DIM), lengths
    ).astype(jnp.bfloat16)
    new_keys = rotary(
        projected_all[:, q_width : q_width + kv_width]
        .astype(jnp.float32)
        .reshape(seq_count, KV_HEADS, HEAD_DIM),
        lengths,
    ).astype(jnp.bfloat16)
    new_values = (
        projected_all[:, q_width + kv_width :]
        .astype(jnp.float32)
        .reshape(seq_count, KV_HEADS, HEAD_DIM)
    )
    pos_count = key_cache.shape[1]
    positions = device_rank * pos_count + jnp.arange(pos_count, dtype=jnp.int32)
    usable = (positions[None, :] < lengths[:, None])[:, None, None, :]
    inverse = 1.0 / math.sqrt(HEAD_DIM)
    grouped = queries.reshape(seq_count, KV_HEADS, groups, HEAD_DIM)
    keys_local = key_cache.reshape(seq_count, pos_count, KV_HEADS, HEAD_DIM)
    values_local = value_cache.reshape(seq_count, pos_count, KV_HEADS, HEAD_DIM).astype(jnp.float32)
    scores = (
        jnp.einsum("bkgd,bpkd->bkgp", grouped, keys_local, preferred_element_type=jnp.float32)
        * inverse
    )
    local_top = jnp.max(jnp.where(usable, scores, -1e30), -1)
    weights = jnp.exp(jnp.where(usable, scores - local_top[..., None], -1e30))
    local_sum = jnp.sum(weights, -1).reshape(seq_count, HEADS)
    local_mix = jnp.einsum("bkgp,bpkd->bkgd", weights, values_local).reshape(
        seq_count, HEADS, HEAD_DIM
    )
    local_top = local_top.reshape(seq_count, HEADS)
    heads_dev = wo.shape[0] // HEAD_DIM
    first_head = device_rank * heads_dev
    tops_in, sums_in, mixes_in = (
        lax.all_to_all(local_top[None], ("tp", "sub"), split_axis=2, concat_axis=0, tiled=True),
        lax.all_to_all(local_sum[None], ("tp", "sub"), split_axis=2, concat_axis=0, tiled=True),
        lax.all_to_all(local_mix[None], ("tp", "sub"), split_axis=2, concat_axis=0, tiled=True),
    )
    best = jnp.max(tops_in, 0)
    factors = jnp.exp(tops_in - best[None])
    head_sum = jnp.sum(sums_in * factors, 0)
    head_mix = jnp.sum(mixes_in * factors[..., None], 0)
    own_queries = lax.dynamic_slice_in_dim(queries, first_head, heads_dev, 1).astype(jnp.float32)
    kv_index = (first_head + jnp.arange(heads_dev, dtype=jnp.int32)) // groups
    own_keys = jnp.take(new_keys, kv_index, axis=1).astype(jnp.float32)
    own_values = jnp.take(new_values, kv_index, axis=1)
    own_score = jnp.sum(own_queries * own_keys, -1) * inverse
    highest = jnp.maximum(best, own_score)
    old_scale = jnp.exp(best - highest)
    own_weight = jnp.exp(own_score - highest)
    numerator = head_mix * old_scale[..., None] + own_weight[..., None] * own_values
    denominator = head_sum * old_scale + own_weight
    attended = (
        (numerator / denominator[..., None])
        .reshape(seq_count, heads_dev * HEAD_DIM)
        .astype(jnp.bfloat16)
    )
    partial_out = jnp.dot(attended, wo, preferred_element_type=jnp.float32)
    summed_out = lax.psum(partial_out, ("tp", "sub"))
    mixed_out = (widened + summed_out).astype(jnp.bfloat16)
    return (mixed_out, new_weight[None, None])


def solution(mesh):
    placed = (
        P("replica", None),
        P("replica"),
        P(("replica", "tp"), "sub", None, None),
        P(("replica", "tp", "sub"), None),
        P("replica", ("tp", "sub"), None),
        P("replica", ("tp", "sub"), None),
        P("replica"),
        P("replica"),
    )
    return jax.shard_map(
        shards,
        mesh=mesh,
        in_specs=placed,
        out_specs=(P("replica", None), P(("replica", "tp"), "sub", None, None)),
        check_vma=False,
    )
```

profile of v0, /device:TPU:8, one launch (start us, length us, event | category | flops | bytes accessed | tf_op | source)
XLA Modules:
  0.0 444.4 jit_solution(11691780571699023312)
XLA Ops:
  7.2 9.9 %constant_dynamic-slice_fusion = (bf16[1,640,4096]{2,1,0:T(8,128)(2,1)}, bf16[640,4096]{1,0:T(8,128)(2,1)}) fusion(bf16[2,640,4096]{2,1,0:T(8,128)(2,1)} %bitcast.145, s32[]{:T(128)S(6)} %select_n.109, s32[]{:T(128)S(6)} %select_n.111), kind=kLoop, calls=%fused_computation.104 | loop fusion | bytes 20971528 | tf_op jit(solution)/shard_map/jit(dynamic_index_in_dim)/dynamic_slice | solution.py:53
  17.1 2.6 collective-permute-start
  19.9 8.3 %copy.49 = bf16[80,8,8,512]{3,2,1,0:T(8,128)(2,1)} copy(bf16[80,8,8,512]{3,1,2,0:T(8,128)(2,1)} %bitcast.144) | data formatting | bytes 10485760
  28.3 0.7 gather_fusion
  29.1 0.2 fusion.17
  29.5 215.0 %collective-permute-done = bf16[640,4096]{1,0:T(8,128)(2,1)} collective-permute-done((bf16[640,4096]{1,0:T(8,128)(2,1)}, bf16[640,4096]{1,0:T(8,128)(2,1)}, u32[]{:S(2)}, u32[]{:S(2)}) %collective-permute-start) | collective-permute-done | bytes 5242912 | tf_op jit(solution)/shard_map/ppermute | solution.py:18
  244.5 6.1 %copy.50 = bf16[80,8,8,512]{3,2,1,0:T(8,128)(2,1)S(1)} copy(bf16[80,8,8,512]{3,1,2,0:T(8,128)(2,1)} %bitcast.49) | data formatting | bytes 10485760
  250.7 5.6 %fusion.3 = bf16[640,512,16]{1,2,0:T(8,128)(2,1)} fusion(bf16[1,640,8,512]{3,2,0,1:T(8,128)(2,1)S(1)} %bitcast.149, bf16[1,640,8,512]{3,2,0,1:T(8,128)(2,1)S(1)} %bitcast.148, s32[16]{0:T(128)S(1)} %and_select_fusion.2), kind=kOutput, calls=%fused_computation.7 | convolution fusion | flops 178258176 | bytes 20971584 | tf_op jit(solution)/shard_map/sa,acr->csr/dot_general | solution.py:70
  256.3 20.5 %copy.51 = bf16[80,8,16,512]{3,1,2,0:T(8,128)(2,1)} copy(bf16[80,8,16,512]{3,2,1,0:T(8,128)(2,1)} %bitcast.141) | data formatting | bytes 20971520
  276.8 6.8 %convolution_convert_fusion = bf16[4,640]{1,0:T(4,128)(2,1)S(1)} fusion(bf16[640,8192]{1,0:T(8,128)(2,1)} %bitcast.143, bf16[4,8192]{1,0:T(4,128)(2,1)S(1)} %copy-done.2, f32[8192]{0:T(1024)S(1)} %copy-done.3, f32[4]{0:T(128)S(1)} %add_rsqrt_fusion), kind=kOutput, calls=%fused_computation.17 | convolution fusion | flops 42076672 | bytes 10589200 | tf_op jit(solution)/shard_map/dot_general | solution.py:75
  283.6 19.8 %all-gather = bf16[4,10240]{1,0:T(4,128)(2,1)S(1)} all-gather(bf16[4,640]{1,0:T(4,128)(2,1)S(1)} %convolution_convert_fusion), channel_id=2, replica_groups=mesh['replica'=2,'tp'=8,'sub'=2] {'tp','sub'}, dimensions={1}, use_global_device_ids=true | all-gather | bytes 87040 | tf_op jit(solution)/shard_map/all_gather | solution.py:78
  303.8 0.8 select_reduce_fusion
  304.6 0.2 fusion.16
  304.8 2.0 fusion.13
  306.8 0.7 copy.45
  307.6 6.6 %all-to-all-start.2 = ((f32[1,4,64]{1,0,2:T(1,128)}), f32[1,4,64]{1,0,2:T(1,128)S(1)}, u32[]{:S(2)}, u32[]{:S(2)}) async-start(f32[1,4,64]{1,0,2:T(1,128)} %bitcast.29), calls=%async_computation.2 | async-start | bytes 65536 | tf_op jit(solution)/shard_map/all_to_all | solution.py:122
  314.3 0.7 copy.37
  315.1 0.6 gather_fusion.1
  315.6 3.6 all-to-all-done.2
  319.3 5.0 %all-to-all-start.1 = ((f32[1,4,64]{1,0,2:T(1,128)}), f32[1,4,64]{1,0,2:T(1,128)S(1)}, u32[]{:S(2)}, u32[]{:S(2)}) async-start(f32[1,4,64]{1,0,2:T(1,128)} %bitcast.16), calls=%async_computation.1 | async-start | bytes 65536 | tf_op jit(solution)/shard_map/all_to_all | solution.py:121
  324.4 0.7 copy.36
  325.3 0.6 gather_fusion.2
  325.8 0.2 copy.46
  326.0 3.3 all-to-all-done.1
  329.4 5.0 %all-to-all-start = ((f32[1,4,64,128]{3,1,0,2:T(4,128)}), f32[1,4,64,128]{3,1,0,2:T(4,128)S(1)}, u32[]{:S(2)}, u32[]{:S(2)}) async-start(f32[1,4,64,128]{3,1,0,2:T(4,128)} %copy.36), calls=%async_computation | async-start | bytes 262144 | tf_op jit(solution)/shard_map/all_to_all | solution.py:123
  334.4 0.2 copy.44
  334.8 0.2 copy.39
  335.1 4.7 %all-to-all-done = f32[1,4,64,128]{3,1,0,2:T(4,128)S(1)} async-done(((f32[1,4,64,128]{3,1,0,2:T(4,128)}), f32[1,4,64,128]{3,1,0,2:T(4,128)S(1)}, u32[]{:S(2)}, u32[]{:S(2)}) %all-to-all-start) | async-done | bytes 131104 | tf_op jit(solution)/shard_map/all_to_all | solution.py:123
  339.9 5.3 %fusion.41 = f32[4,8192]{1,0:T(4,128)} fusion(bf16[512,8192]{1,0:T(8,128)(2,1)} %param.11, f32[1,4,4,128]{3,2,1,0:T(4,128)S(1)} %broadcast_bitcast_fusion, f32[4,4,128]{2,1,0:T(4,128)S(1)} %gather_fusion.2, f32[1,4,4,128]{3,2,1,0:T(4,128)S(1)} %broadcast_bitcast_fusion.1, f32[4,4,128]{2,0,1:T(4,128)S(1)} %multiply_reduce_fusion, f32[4,4]{0,1:T(4,128)S(1)} %copy.41, ...), kind=kOutput, calls=%fused_computation.69 | convolution fusion | flops 33566720 | bytes 8553024 | tf_op jit(solution)/shard_map/dot_general | solution.py:144
  345.2 16.5 %broadcast_in_dim_reshape.15 = bf16[1,1,640,8192]{3,2,1,0:T(8,128)(2,1)} reshape(bf16[640,16,512]{2,1,0:T(8,128)(2,1)} %bitcast.142) | data formatting | bytes 20971520 | tf_op jit(solution)/shard_map/broadcast_in_dim;reshape | solution.py:147
  361.7 74.2 %all-reduce.2.cloned.1.call-done = f32[4,8192]{1,0:T(4,128)} async-done(((f32[4,8192]{1,0:T(4,128)}), f32[4,8192]{1,0:T(4,128)}) %all-reduce.2.cloned.1.call-update) | async-done | bytes 131088 | tf_op jit(solution)/shard_map/psum | solution.py:145
  435.9 1.6 fusion.20
  (52 shorter events, 1.8 us)
Async XLA Ops:
  7.2 296.6 %copy-start = (bf16[4,256,1024]{2,1,0:T(8,128)(2,1)S(1)}, bf16[4,256,1024]{2,1,0:T(8,128)(2,1)}, u32[]{:S(2)}) copy-start(bf16[4,256,1024]{2,1,0:T(8,128)(2,1)} %param.12) | copy-start | bytes 6291460
  17.1 227.4 %collective-permute-start = (bf16[640,4096]{1,0:T(8,128)(2,1)}, bf16[640,4096]{1,0:T(8,128)(2,1)}, u32[]{:S(2)}, u32[]{:S(2)}) collective-permute-start(bf16[640,4096]{1,0:T(8,128)(2,1)} %get-tuple-element.8), channel_id=1, source_target_pairs={{0,8},{2,10},{4,12},{6,14},{8,0},{10,2},{12,4},{14,6},{1,9},{3,11}... | collective-permute-start | bytes 15728648 | tf_op jit(solution)/shard_map/ppermute | solution.py:18
  19.9 8.4 %copy-start.4 = (s32[4]{0:T(128)S(1)}, s32[4]{0:T(128)}, u32[]{:S(2)}) copy-start(s32[4]{0:T(128)} %param.14) | copy-start | bytes 52
  19.9 8.4 %copy-start.1 = (s32[16]{0:T(128)S(1)}, s32[16]{0:T(128)}, u32[]{:S(2)}) copy-start(s32[16]{0:T(128)} %param.15) | copy-start | bytes 196
  19.9 9.1 %copy-start.2 = (bf16[4,8192]{1,0:T(4,128)(2,1)S(1)}, bf16[4,8192]{1,0:T(4,128)(2,1)}, u32[]{:S(2)}) copy-start(bf16[4,8192]{1,0:T(4,128)(2,1)} %param.8) | copy-start | bytes 196612
  28.3 222.4 %slice-start = ((s8[5242880]{0:T(1024)(128)(4,1)}), s8[1048576]{0:T(1024)(128)(4,1)S(1)}, s32[]{:S(2)}) async-start(s8[5242880]{0:T(1024)(128)(4,1)} %bitcast.146), calls=%async_computation.4 | async-start | bytes 2097152
  244.5 6.1 %slice-start.1 = ((s8[5242880]{0:T(1024)(128)(4,1)}), s8[4194304]{0:T(1024)(128)(4,1)S(1)}, s32[]{:S(2)}) async-start(s8[5242880]{0:T(1024)(128)(4,1)} %bitcast.146), calls=%async_computation.5 | async-start | bytes 8388608
  256.3 20.6 %copy-start.3 = (f32[8192]{0:T(1024)S(1)}, f32[8192]{0:T(1024)}, u32[]{:S(2)}) copy-start(f32[8192]{0:T(1024)} %param.9) | copy-start | bytes 98308
  307.6 11.7 %all-to-all-start.2 = ((f32[1,4,64]{1,0,2:T(1,128)}), f32[1,4,64]{1,0,2:T(1,128)S(1)}, u32[]{:S(2)}, u32[]{:S(2)}) async-start(f32[1,4,64]{1,0,2:T(1,128)} %bitcast.29), calls=%async_computation.2 | async-start | bytes 65536 | tf_op jit(solution)/shard_map/all_to_all | solution.py:122
  319.3 10.1 %all-to-all-start.1 = ((f32[1,4,64]{1,0,2:T(1,128)}), f32[1,4,64]{1,0,2:T(1,128)S(1)}, u32[]{:S(2)}, u32[]{:S(2)}) async-start(f32[1,4,64]{1,0,2:T(1,128)} %bitcast.16), calls=%async_computation.1 | async-start | bytes 65536 | tf_op jit(solution)/shard_map/all_to_all | solution.py:121
  329.4 10.4 %all-to-all-start = ((f32[1,4,64,128]{3,1,0,2:T(4,128)}), f32[1,4,64,128]{3,1,0,2:T(4,128)S(1)}, u32[]{:S(2)}, u32[]{:S(2)}) async-start(f32[1,4,64,128]{3,1,0,2:T(4,128)} %copy.36), calls=%async_computation | async-start | bytes 262144 | tf_op jit(solution)/shard_map/all_to_all | solution.py:123
  334.4 101.6 %all-reduce.2.cloned.1.call-start = ((), (), s32[]{:S(2)}) async-start(), calls=%async_computation.3 | async-start | bytes 262144 | tf_op jit(solution)/shard_map/psum | solution.py:145
Sparse Core Ops, SparseCore 0:
  345.4 90.5 all-reduce.1
where the time goes:
time: 445 us; the launch traced here: 444 us
  waiting for transfers between devices  301 us (68%)
  local copies, waits for them, and re-layouts  66.7 us (15%)
  matrix products  20.4 us (5%)
  blocking collectives  19.8 us (4%)
  starting transfers between devices  19.2 us (4%)
  between operations  14.3 us (3%)
    ppermute x1, waiting for transfers between devices, passed_along(): return lax.ppermute(value, axis, pairs)  215 us
    psum x1, waiting for transfers between devices, shards(): summed_out = lax.psum(partial_out, ('tp', 'sub'))  74.2 us
    unnamed x20, local copies, waits for them, and re-layouts  35.2 us
    all_gather x1, blocking collectives, shards(): lax.all_gather(projected[:, None, :], ('tp', 'sub'), axis=1, tiled=True)  19.8 us
    another operation x1, local copies, waits for them, and re-layouts, shards(): return (mixed_out, new_weight[None, None])  16.5 us
    dynamic_slice x1, local copies, waits for them, and re-layouts, shards(): lax.dynamic_index_in_dim(old_block, own_section, 0, keepdims=False)  9.85 us
  transfers between devices with their start and end apart: 5, of which 5 were waited for; matrix products, arithmetic and copies ran while one was open for 7% of the time, Pallas kernels for 0%

commit v1 on v0

--- a/solution.py
+++ b/solution.py
@@ -3,13 +3,18 @@
 import jax
 import jax.numpy as jnp
 from jax import lax
+from jax.experimental import pallas as pl
+from jax.experimental.pallas import tpu as pltpu
 from jax.sharding import PartitionSpec as P
+
 
 HEADS = 64
 KV_HEADS = 8
 HEAD_DIM = 128
 RANKS = 8
 ROW_BLOCKS = 16
+CHUNKS = 16
+WAVE_STARTS = (0, 2, 5, 8, 11)
 
 
 def passed_along(value, axis, steps):
@@ -37,8 +42,84 @@
     return (widened, (widened * factor * norm_gain).astype(jnp.bfloat16))
 
 
+def cut_rows(targets, weight, offset, chunk, rows):
+    def kernel(target_ref, weight_ref, out_ref):
+        out_ref[...] = weight_ref[...]
+
+    shape = (1, 1, rows, weight.shape[3])
+    return pl.pallas_call(
+        kernel,
+        out_shape=jax.ShapeDtypeStruct(shape, weight.dtype),
+        grid_spec=pltpu.PrefetchScalarGridSpec(
+            num_scalar_prefetch=1,
+            grid=(1,),
+            in_specs=[
+                pl.BlockSpec(shape, lambda step, target_ref: (0, 0, target_ref[offset] + chunk, 0))
+            ],
+            out_specs=pl.BlockSpec(shape, lambda step, target_ref: (0, 0, 0, 0)),
+        ),
+        cost_estimate=pl.CostEstimate(
+            flops=0, bytes_accessed=4 * rows * weight.shape[3], transcendentals=0
+        ),
+    )(targets, weight)
+
+
+def placed_blocks(slots, data, dest, full_shape, offset, per, rows, first_row):
+    last = slots.shape[0] - 1
+    width = data.shape[-1] // per
+    steps = 1 if dest is not None else full_shape[2] // rows
+
+    def kernel(slot_ref, data_ref, *rest):
+        out_ref, sems = rest[-2:]
+        step = pl.program_id(0)
+        at_row = pl.multiple_of(first_row + step * rows, 8)
+        copies = []
+        for block in range(per):
+            column = pl.multiple_of(slot_ref[offset * per + block] * width, width)
+            copies.append(
+                pltpu.make_async_copy(
+                    data_ref.at[0, 0, :, pl.ds(block * width, width)],
+                    out_ref.at[0, 0, pl.ds(at_row, rows), pl.ds(column, width)],
+                    sems.at[block],
+                )
+            )
+        for copy in copies:
+            copy.start()
+        for copy in copies:
+            copy.wait()
+
+    moved = 2 * steps * rows * data.shape[-1] * 2
+    in_specs = [
+        pl.BlockSpec(
+            (1, 1, rows, data.shape[-1]),
+            lambda step, slot_ref: (0, 0, 0 if dest is not None else slot_ref[last] + step, 0),
+        )
+    ]
+    operands = [slots, data]
+    aliases = {}
+    if dest is not None:
+        in_specs.append(pl.BlockSpec(memory_space=pl.ANY))
+        operands.append(dest)
+        aliases = {2: 0}
+    return pl.pallas_call(
+        kernel,
+        out_shape=jax.ShapeDtypeStruct(full_shape, data.dtype),
+        grid_spec=pltpu.PrefetchScalarGridSpec(
+            num_scalar_prefetch=1,
+            grid=(steps,),
+            in_specs=in_specs,
+            out_specs=pl.BlockSpec(memory_space=pl.ANY),
+            scratch_shapes=[pltpu.SemaphoreType.DMA((per,))],
+        ),
+        input_output_aliases=aliases,
+        cost_estimate=pl.CostEstimate(flops=0, bytes_accessed=moved, transcendentals=0),
+    )(*operands)
+
+
 def shards(hidden_in, norm_gain, wqkv_old, wo, key_cache, value_cache, lengths, section_order):
     tp_count = lax.axis_size("tp")
+    sub_count = lax.axis_size("sub")
+    device_count = tp_count * sub_count
     section_count = tp_count // 4
     per_section = ROW_BLOCKS // section_count
     tp_index = lax.axis_index("tp")
@@ -48,38 +129,44 @@
     cols_dev = wqkv_old.shape[2] // section_count
     rows_old = wqkv_old.shape[3]
     block_rows = rows_old // per_section
-    old_block = wqkv_old[0, 0].reshape(section_count, cols_dev, rows_old)
-    slot_ids = jnp.arange(section_count, dtype=jnp.int32)
-    arrived = [lax.dynamic_index_in_dim(old_block, own_section, 0, keepdims=False)]
-    for offset in range(1, section_count):
-        outgoing = lax.dynamic_index_in_dim(
-            old_block, (own_section + offset) % section_count, 0, keepdims=False
-        )
-        arrived.append(passed_along(outgoing, "tp", 4 * offset))
-    received = jnp.stack(arrived, 0)
-    sources = (own_section - slot_ids) % section_count
-    block_ids = jnp.arange(ROW_BLOCKS, dtype=jnp.int32)
-    local_source = (
-        sources[:, None] * per_section + jnp.arange(per_section, dtype=jnp.int32)[None, :]
-    ).reshape(ROW_BLOCKS)
-    target_block = jnp.take(section_order, local_source, axis=0)
-    placing = (target_block[None, :] == block_ids[:, None]).astype(jnp.bfloat16)
-    received_blocks = jnp.transpose(
-        received.reshape(section_count, cols_dev, per_section, block_rows), (0, 2, 1, 3)
-    ).reshape(ROW_BLOCKS, cols_dev, block_rows)
-    new_weight = jnp.einsum(
-        "sa,acr->csr", placing, received_blocks, preferred_element_type=jnp.float32
-    ).astype(jnp.bfloat16)
-    new_weight = new_weight.reshape(cols_dev, ROW_BLOCKS * block_rows)
-    widened, normed = rms_normed(hidden_in, norm_gain)
-    projected = lax.dot_general(
-        normed, new_weight, (((1,), (1,)), ((), ())), preferred_element_type=jnp.float32
-    ).astype(jnp.bfloat16)
-    gathered = lax.all_gather(projected[:, None, :], ("tp", "sub"), axis=1, tiled=True)
-    seq_count = hidden_in.shape[0]
-    projected_all = jnp.transpose(
-        gathered.reshape(seq_count, section_count, RANKS, cols_dev), (0, 2, 1, 3)
-    ).reshape(seq_count, -1)
+    seq_count, width = hidden_in.shape
+
+    chunks = max(1, CHUNKS // max(1, section_count - 1))
+    chunk_rows = cols_dev // chunks
+    pieces = [(offset, chunk) for chunk in range(chunks) for offset in range(1, section_count)]
+    arrived = []
+
+    targets = (own_section + jnp.arange(section_count, dtype=jnp.int32)) % section_count * chunks
+
+    def send_wave(wave):
+        first = WAVE_STARTS[wave]
+        last = WAVE_STARTS[wave + 1] if wave + 1 < len(WAVE_STARTS) else len(pieces)
+        for index in range(first, last):
+            offset, chunk = pieces[index]
+            outgoing = cut_rows(targets, wqkv_old, offset, chunk, chunk_rows)
+            arrived.append((offset, chunk, passed_along(outgoing, "tp", 4 * offset)))
+
+    def exchanged(blocks):
+        return lax.all_to_all(blocks, ("tp", "sub"), split_axis=0, concat_axis=0, tiled=True)
+
+    send_wave(0)
+
+    _, normed = rms_normed(hidden_in, norm_gain)
+    own_slots = lax.dynamic_slice_in_dim(section_order, own_section * per_section, per_section)
+    own_rows = jnp.take(normed.reshape(seq_count, ROW_BLOCKS, block_rows), own_slots, axis=1)
+    partial_units = lax.dot_general(
+        own_rows.reshape(seq_count, rows_old),
+        wqkv_old[0, 0],
+        (((1,), (1,)), ((), ())),
+        preferred_element_type=jnp.float32,
+    )
+    send_wave(1)
+    gathered = exchanged(
+        jnp.broadcast_to(partial_units[None], (device_count,) + partial_units.shape)
+    )
+    units = jnp.sum(gathered.reshape(section_count, RANKS, seq_count, -1), 0).astype(jnp.bfloat16)
+    projected_all = jnp.transpose(units, (1, 0, 2)).reshape(seq_count, -1)
+
     q_width = HEADS * HEAD_DIM
     kv_width = KV_HEADS * HEAD_DIM
     groups = HEADS // KV_HEADS
@@ -117,11 +204,25 @@
     local_top = local_top.reshape(seq_count, HEADS)
     heads_dev = wo.shape[0] // HEAD_DIM
     first_head = device_rank * heads_dev
-    tops_in, sums_in, mixes_in = (
-        lax.all_to_all(local_top[None], ("tp", "sub"), split_axis=2, concat_axis=0, tiled=True),
-        lax.all_to_all(local_sum[None], ("tp", "sub"), split_axis=2, concat_axis=0, tiled=True),
-        lax.all_to_all(local_mix[None], ("tp", "sub"), split_axis=2, concat_axis=0, tiled=True),
-    )
+    half = HEAD_DIM // 2
+    spread = (seq_count, HEADS, half)
+    packed = jnp.concatenate(
+        [
+            local_mix,
+            jnp.broadcast_to(local_top[..., None], spread),
+            jnp.broadcast_to(local_sum[..., None], spread),
+        ],
+        -1,
+    )
+    packed = jnp.transpose(
+        packed.reshape(seq_count, device_count, heads_dev, 2 * HEAD_DIM), (1, 0, 2, 3)
+    ).reshape(device_count, seq_count * heads_dev, 2 * HEAD_DIM)
+    send_wave(2)
+    parts_in = exchanged(packed)
+    parts_in = parts_in.reshape(device_count, seq_count, heads_dev, 2 * HEAD_DIM)
+    mixes_in = parts_in[..., :HEAD_DIM]
+    tops_in = parts_in[..., HEAD_DIM]
+    sums_in = parts_in[..., HEAD_DIM + half]
     best = jnp.max(tops_in, 0)
     factors = jnp.exp(tops_in - best[None])
     head_sum = jnp.sum(sums_in * factors, 0)
@@ -142,9 +243,39 @@
         .astype(jnp.bfloat16)
     )
     partial_out = jnp.dot(attended, wo, preferred_element_type=jnp.float32)
-    summed_out = lax.psum(partial_out, ("tp", "sub"))
-    mixed_out = (widened + summed_out).astype(jnp.bfloat16)
-    return (mixed_out, new_weight[None, None])
+    share = width // device_count
+    by_owner = jnp.transpose(partial_out.reshape(seq_count, device_count, share), (1, 0, 2))
+    send_wave(3)
+    shares_in = exchanged(by_owner)
+    own_hidden = lax.dynamic_slice_in_dim(hidden_in, device_rank * share, share, 1)
+    own_out = (own_hidden.astype(jnp.float32) + jnp.sum(shares_in, 0)).astype(jnp.bfloat16)
+    send_wave(4)
+    all_out = exchanged(jnp.broadcast_to(own_out[None], (device_count,) + own_out.shape))
+    mixed_out = jnp.transpose(all_out, (1, 0, 2)).reshape(seq_count, width)
+
+    full_shape = (1, 1, cols_dev, ROW_BLOCKS * block_rows)
+    sources = (own_section - jnp.arange(section_count, dtype=jnp.int32)) % section_count
+    slots = jnp.concatenate(
+        [
+            jnp.take(section_order.reshape(section_count, per_section), sources, axis=0).reshape(-1),
+            (own_section * chunks)[None].astype(jnp.int32),
+        ]
+    )
+    new_weight = placed_blocks(
+        slots, wqkv_old, None, full_shape, 0, per_section, chunk_rows, 0
+    )
+    for offset, chunk, data in arrived:
+        new_weight = placed_blocks(
+            slots,
+            data,
+            new_weight,
+            full_shape,
+            offset,
+            per_section,
+            chunk_rows,
+            chunk * chunk_rows,
+        )
+    return (mixed_out, new_weight)
 
 
 def solution(mesh):
@@ -158,6 +289,7 @@
         P("replica"),
         P("replica"),
     )
+
     return jax.shard_map(
         shards,
         mesh=mesh,

time: 445 us -> 312 us (0.70)
  waiting for transfers between devices: 301 us -> 116 us
  Pallas kernels: 0 us -> 93 us
  local copies, waits for them, and re-layouts: 66.7 us -> 21 us
  starting transfers between devices: 19.2 us -> 56 us
  blocking collectives: 19.8 us -> 0 us
  between operations: 14.3 us -> 1.1 us
  matrix products: 20.4 us -> 15.9 us
    ppermute x1 -> x16, waiting for transfers between devices: 215 us -> 75.3 us  [passed_along(): return lax.ppermute(value, axis, pairs)]
    pallas_call x0 -> x33, Pallas kernels: none -> 93 us  [the longest x17 54.4 us: placed_blocks(): pl.pallas_call(kernel, out_shape=jax.ShapeDtypeStruct(full_shape, data.dt...]
    psum x1 -> x0, waiting for transfers between devices: 74.2 us -> none  [shards(): summed_out = lax.psum(partial_out, ('tp', 'sub'))]
    unnamed x20 -> x23, local copies, waits for them, and re-layouts: 35.2 us -> 0.74 us
    ppermute x1 -> x16, starting transfers between devices: 2.59 us -> 35.7 us  [passed_along(): return lax.ppermute(value, axis, pairs)]
    all_to_all x3 -> x4, waiting for transfers between devices: 11.6 us -> 40.4 us  [exchanged(): lax.all_to_all(blocks, ('tp', 'sub'), split_axis=0, concat_axis=0, tiled=...]
    all_gather x1 -> x0, blocking collectives: 19.8 us -> none  [shards(): lax.all_gather(projected[:, None, :], ('tp', 'sub'), axis=1, tiled=True)]
    another operation x3 -> x0, local copies, waits for them, and re-layouts: 18 us -> none  [the longest x1 16.5 us: shards(): return (mixed_out, new_weight[None, None])]
  transfers between devices with their start and end apart: 5 -> 20, of which waited for: 5 -> 7; matrix products, arithmetic and copies ran while one was open for 7% -> 14% of each run, Pallas kernels for 0% -> 29%
where the time goes in v1:
time: 312 us; the launch traced here: 310 us
  waiting for transfers between devices  116 us (37%)
  Pallas kernels  93 us (30%)
  starting transfers between devices  56 us (18%)
  local copies, waits for them, and re-layouts  21 us (7%)
  matrix products  15.9 us (5%)
  other arithmetic  7.24 us (2%)
    ppermute x16, waiting for transfers between devices, passed_along(): return lax.ppermute(value, axis, pairs)  75.3 us
    pallas_call x17, Pallas kernels, placed_blocks(): pl.pallas_call(kernel, out_shape=jax.ShapeDtypeStruct(full_shape, data.dt...  54.4 us
    all_to_all x4, waiting for transfers between devices, exchanged(): lax.all_to_all(blocks, ('tp', 'sub'), split_axis=0, concat_axis=0, tiled=...  40.4 us
    pallas_call x16, Pallas kernels, cut_rows(): pl.pallas_call(kernel, out_shape=jax.ShapeDtypeStruct(shape, weight.dtype...  38.6 us
    ppermute x16, starting transfers between devices, passed_along(): return lax.ppermute(value, axis, pairs)  35.7 us
    all_to_all x4, starting transfers between devices, exchanged(): lax.all_to_all(blocks, ('tp', 'sub'), split_axis=0, concat_axis=0, tiled=...  20.3 us
    dot_general x1, local copies, waits for them, and re-layouts, shards(): partial_out = jnp.dot(attended, wo, preferred_element_type=jnp.float32)  11.9 us
    dot_general x1, matrix products, shards(): lax.dot_general(own_rows.reshape(seq_count, rows_old), wqkv_old[0, 0], ((...  6.78 us
  transfers between devices with their start and end apart: 20, of which 7 were waited for; matrix products, arithmetic and copies ran while one was open for 14% of the time, Pallas kernels for 29%

profile of v1, /device:TPU:8, one launch (start us, length us, event | category | flops | bytes accessed | tf_op | source)
XLA Modules:
  0.0 309.8 jit_solution(8960657811679366545)
XLA Ops:
  1.2 2.5 shard_map.110
  3.7 2.6 collective-permute-start.15
  11.4 2.6 collective-permute-start.13
  19.1 2.6 collective-permute-start.11
  22.8 6.8 %fusion = f32[4,1280]{1,0:T(4,128)S(1)} fusion(bf16[4,4096]{1,0:T(4,128)(2,1)S(1)} %bitcast.117, bf16[1,1,1280,4096]{3,2,1,0:T(8,128)(2,1)} %data_ref.1), kind=kOutput, calls=%fused_computation.4 | convolution fusion | flops 41943040 | bytes 10539008 | tf_op jit(solution)/shard_map/dot_general | solution.py:157
  30.3 4.3 %all-to-all-start = ((f32[16,4,1280]{2,1,0:T(4,128)}), f32[16,4,1280]{2,1,0:T(4,128)S(1)}, u32[]{:S(2)}, u32[]{:S(2)}) async-start(f32[16,4,1280]{2,1,0:T(4,128)} %broadcast_in_dim.104), calls=%async_computation | async-start | bytes 655360 | tf_op jit(solution)/shard_map/all_to_all | solution.py:150
  37.1 11.9 %copy.126 = bf16[8192,512]{1,0:T(8,128)(2,1)} copy(bf16[8192,512]{0,1:T(8,128)(2,1)} %bitcast.104) | data formatting | bytes 16777216 | tf_op jit(solution)/shard_map/dot_general | solution.py:245
  49.2 34.4 %all-to-all-done = f32[16,4,1280]{2,1,0:T(4,128)S(1)} async-done(((f32[16,4,1280]{2,1,0:T(4,128)}), f32[16,4,1280]{2,1,0:T(4,128)S(1)}, u32[]{:S(2)}, u32[]{:S(2)}) %all-to-all-start) | async-done | bytes 327712 | tf_op jit(solution)/shard_map/all_to_all | solution.py:150
  88.5 6.9 %all-to-all-start.1 = ((f32[16,16,256]{2,1,0:T(8,128)}), f32[16,16,256]{2,1,0:T(8,128)S(1)}, u32[]{:S(2)}, u32[]{:S(2)}) async-start(f32[16,16,256]{2,1,0:T(8,128)} %copy.115), calls=%async_computation.1 | async-start | bytes 524288 | tf_op jit(solution)/shard_map/all_to_all | solution.py:150
  97.0 6.0 %all-to-all-done.1 = f32[16,16,256]{2,1,0:T(8,128)S(1)} async-done(((f32[16,16,256]{2,1,0:T(8,128)}), f32[16,16,256]{2,1,0:T(8,128)S(1)}, u32[]{:S(2)}, u32[]{:S(2)}) %all-to-all-start.1) | async-done | bytes 262176 | tf_op jit(solution)/shard_map/all_to_all | solution.py:150
  103.0 2.5 copy.116
  112.5 6.3 %convolution_bitcast_fusion = f32[16,4,512]{2,1,0:T(4,128)} fusion(bf16[16,512,512]{2,1,0:T(8,128)(2,1)} %bitcast.103, f32[4,4,128]{2,1,0:T(4,128)S(1)} %gather_fusion.2, f32[4,4,128]{2,0,1:T(4,128)S(1)} %copy.120, f32[4,4]{0,1:T(4,128)S(1)} %copy.122, f32[4,4]{0,1:T(4,128)S(1)} %copy.121, f32[4,4]{0,1:T(4,128)S(1)} %copy.119, ...), kind=kOutput, calls=%fused_computation.13 | convolution fusion | flops 33566720 | bytes 8536260 | tf_op jit(solution)/shard_map/dot_general | solution.py:245
  118.8 4.9 %all-to-all-start.2 = ((f32[16,4,512]{2,1,0:T(4,128)}), f32[16,4,512]{2,1,0:T(4,128)S(1)}, u32[]{:S(2)}, u32[]{:S(2)}) async-start(f32[16,4,512]{2,1,0:T(4,128)} %convolution_bitcast_fusion), calls=%async_computation.2 | async-start | bytes 262144 | tf_op jit(solution)/shard_map/all_to_all | solution.py:150
  142.8 2.5 shard_map.96
  145.4 2.5 shard_map.95
  148.4 2.5 collective-permute-start.9
  157.5 4.2 %all-to-all-start.3 = ((bf16[16,4,512]{2,1,0:T(4,128)(2,1)}), bf16[16,4,512]{2,1,0:T(4,128)(2,1)S(1)}, u32[]{:S(2)}, u32[]{:S(2)}) async-start(bf16[16,4,512]{2,1,0:T(4,128)(2,1)} %broadcast_in_dim.113), calls=%async_computation.3 | async-start | bytes 131072 | tf_op jit(solution)/shard_map/all_to_all | solution.py:150
  161.8 32.6 %collective-permute-done.9.data_ref = bf16[1,1,40,4096]{3,2,1,0:T(8,128)(2,1)} collective-permute-done((bf16[1,1,40,4096]{3,2,1,0:T(8,128)(2,1)}, bf16[1,1,40,4096]{3,2,1,0:T(8,128)(2,1)}, u32[]{:S(2)}, u32[]{:S(2)}) %collective-permute-start.9) | collective-permute-done | bytes 327712 | tf_op jit(solution)/shard_map/ppermute | solution.py:23
  194.4 3.4 %collective-permute-start.4 = (bf16[1,1,40,4096]{3,2,1,0:T(8,128)(2,1)}, bf16[1,1,40,4096]{3,2,1,0:T(8,128)(2,1)}, u32[]{:S(2)}, u32[]{:S(2)}) collective-permute-start(bf16[1,1,40,4096]{3,2,1,0:T(8,128)(2,1)} %shard_map.99), channel_id=1, source_target_pairs={{0,8},{2,10},{4,12},{6,14},{8,0},{10,2},{12,4},{14,6},{1,9},{3,11}... | collective-permute-start | bytes 983048 | tf_op jit(solution)/shard_map/ppermute | solution.py:23
  197.7 10.7 %collective-permute-done.8.data_ref = bf16[1,1,40,4096]{3,2,1,0:T(8,128)(2,1)} collective-permute-done((bf16[1,1,40,4096]{3,2,1,0:T(8,128)(2,1)}, bf16[1,1,40,4096]{3,2,1,0:T(8,128)(2,1)}, u32[]{:S(2)}, u32[]{:S(2)}) %collective-permute-start.8) | collective-permute-done | bytes 327712 | tf_op jit(solution)/shard_map/ppermute | solution.py:23
  208.4 3.4 %collective-permute-start.3 = (bf16[1,1,40,4096]{3,2,1,0:T(8,128)(2,1)}, bf16[1,1,40,4096]{3,2,1,0:T(8,128)(2,1)}, u32[]{:S(2)}, u32[]{:S(2)}) collective-permute-start(bf16[1,1,40,4096]{3,2,1,0:T(8,128)(2,1)} %shard_map.98), channel_id=1, source_target_pairs={{0,8},{2,10},{4,12},{6,14},{8,0},{10,2},{12,4},{14,6},{1,9},{3,11}... | collective-permute-start | bytes 983048 | tf_op jit(solution)/shard_map/ppermute | solution.py:23
  211.8 10.7 %collective-permute-done.7.data_ref = bf16[1,1,40,4096]{3,2,1,0:T(8,128)(2,1)} collective-permute-done((bf16[1,1,40,4096]{3,2,1,0:T(8,128)(2,1)}, bf16[1,1,40,4096]{3,2,1,0:T(8,128)(2,1)}, u32[]{:S(2)}, u32[]{:S(2)}) %collective-permute-start.7) | collective-permute-done | bytes 327712 | tf_op jit(solution)/shard_map/ppermute | solution.py:23
  222.4 3.4 %collective-permute-start.2 = (bf16[1,1,40,4096]{3,2,1,0:T(8,128)(2,1)S(1)}, bf16[1,1,40,4096]{3,2,1,0:T(8,128)(2,1)}, u32[]{:S(2)}, u32[]{:S(2)}) collective-permute-start(bf16[1,1,40,4096]{3,2,1,0:T(8,128)(2,1)S(1)} %copy-done.3), channel_id=1, source_target_pairs={{0,8},{2,10},{4,12},{6,14},{8,0},{10,2},{12,4},{14,6},{1,9},{3,11}... | collective-permute-start | bytes 983048 | tf_op jit(solution)/shard_map/ppermute | solution.py:23
  225.8 10.7 %collective-permute-done.6.data_ref = bf16[1,1,40,4096]{3,2,1,0:T(8,128)(2,1)} collective-permute-done((bf16[1,1,40,4096]{3,2,1,0:T(8,128)(2,1)}, bf16[1,1,40,4096]{3,2,1,0:T(8,128)(2,1)}, u32[]{:S(2)}, u32[]{:S(2)}) %collective-permute-start.6) | collective-permute-done | bytes 327712 | tf_op jit(solution)/shard_map/ppermute | solution.py:23
  236.5 3.4 %collective-permute-start.1 = (bf16[1,1,40,4096]{3,2,1,0:T(8,128)(2,1)S(1)}, bf16[1,1,40,4096]{3,2,1,0:T(8,128)(2,1)}, u32[]{:S(2)}, u32[]{:S(2)}) collective-permute-start(bf16[1,1,40,4096]{3,2,1,0:T(8,128)(2,1)S(1)} %copy-done.2), channel_id=1, source_target_pairs={{0,8},{2,10},{4,12},{6,14},{8,0},{10,2},{12,4},{14,6},{1,9},{3,11}... | collective-permute-start | bytes 983048 | tf_op jit(solution)/shard_map/ppermute | solution.py:23
  239.9 10.7 %collective-permute-done.5.data_ref = bf16[1,1,40,4096]{3,2,1,0:T(8,128)(2,1)S(1)} collective-permute-done((bf16[1,1,40,4096]{3,2,1,0:T(8,128)(2,1)}, bf16[1,1,40,4096]{3,2,1,0:T(8,128)(2,1)S(1)}, u32[]{:S(2)}, u32[]{:S(2)}) %collective-permute-start.5) | collective-permute-done | bytes 327712 | tf_op jit(solution)/shard_map/ppermute | solution.py:23
  250.5 3.3 %collective-permute-start = (bf16[1,1,40,4096]{3,2,1,0:T(8,128)(2,1)}, bf16[1,1,40,4096]{3,2,1,0:T(8,128)(2,1)}, u32[]{:S(2)}, u32[]{:S(2)}) collective-permute-start(bf16[1,1,40,4096]{3,2,1,0:T(8,128)(2,1)} %shard_map.95), channel_id=1, source_target_pairs={{0,8},{2,10},{4,12},{6,14},{8,0},{10,2},{12,4},{14,6},{1,9},{3,11}... | collective-permute-start | bytes 983048 | tf_op jit(solution)/shard_map/ppermute | solution.py:23
  254.5 15.7 %shard_map.111.rest_0_ = bf16[1,1,640,8192]{3,2,1,0:T(8,128)(2,1)} custom-call(s32[17]{0:T(128)} %pad_add_fusion.slot_ref, bf16[1,1,1280,4096]{3,2,1,0:T(8,128)(2,1)} %data_ref.1), custom_call_target="tpu_custom_call" | custom-call | bytes 10485760 | tf_op jit(solution)/shard_map/pallas_call | solution.py:104
  277.5 2.4 shard_map.115.rest_0_
  280.0 2.4 shard_map.116.rest_0_
  282.4 2.4 shard_map.117.rest_0_
  292.1 2.4 shard_map.121.rest_0_
  (128 shorter events, 85.3 us)
Async XLA Ops:
  0.6 83.3 %copy-start = (bf16[4,256,1024]{2,1,0:T(8,128)(2,1)S(1)}, bf16[4,256,1024]{2,1,0:T(8,128)(2,1)}, u32[]{:S(2)}) copy-start(bf16[4,256,1024]{2,1,0:T(8,128)(2,1)} %param.12) | copy-start | bytes 6291460
  3.7 106.6 %collective-permute-start.15 = (bf16[1,1,40,4096]{3,2,1,0:T(8,128)(2,1)}, bf16[1,1,40,4096]{3,2,1,0:T(8,128)(2,1)S(1)}, u32[]{:S(2)}, u32[]{:S(2)}) collective-permute-start(bf16[1,1,40,4096]{3,2,1,0:T(8,128)(2,1)} %shard_map.110), channel_id=1, source_target_pairs={{0,8},{2,10},{4,12},{6,14},{8,0},{10,2},{12,4},{14,6},{1,9},{3,11}... | collective-permute-start | bytes 983048 | tf_op jit(solution)/shard_map/ppermute | solution.py:23
  8.7 139.8 %collective-permute-start.14 = (bf16[1,1,40,4096]{3,2,1,0:T(8,128)(2,1)}, bf16[1,1,40,4096]{3,2,1,0:T(8,128)(2,1)}, u32[]{:S(2)}, u32[]{:S(2)}) collective-permute-start(bf16[1,1,40,4096]{3,2,1,0:T(8,128)(2,1)} %shard_map.109), channel_id=1, source_target_pairs={{0,8},{2,10},{4,12},{6,14},{8,0},{10,2},{12,4},{14,6},{1,9},{3,11}... | collective-permute-start | bytes 983048 | tf_op jit(solution)/shard_map/ppermute | solution.py:23
  11.4 10.3 %copy-start.9 = (s32[16]{0:T(128)S(1)}, s32[16]{0:T(128)}, u32[]{:S(2)}) copy-start(s32[16]{0:T(128)} %param.15) | copy-start | bytes 196
  11.4 10.4 %copy-start.6 = (bf16[4,8192]{1,0:T(4,128)(2,1)S(1)}, bf16[4,8192]{1,0:T(4,128)(2,1)}, u32[]{:S(2)}) copy-start(bf16[4,8192]{1,0:T(4,128)(2,1)} %param.8) | copy-start | bytes 196612
  11.4 10.6 %copy-start.7 = (f32[8192]{0:T(1024)S(1)}, f32[8192]{0:T(1024)}, u32[]{:S(2)}) copy-start(f32[8192]{0:T(1024)} %param.9) | copy-start | bytes 98308
  11.4 139.5 %collective-permute-start.13 = (bf16[1,1,40,4096]{3,2,1,0:T(8,128)(2,1)}, bf16[1,1,40,4096]{3,2,1,0:T(8,128)(2,1)}, u32[]{:S(2)}, u32[]{:S(2)}) collective-permute-start(bf16[1,1,40,4096]{3,2,1,0:T(8,128)(2,1)} %shard_map.108), channel_id=1, source_target_pairs={{0,8},{2,10},{4,12},{6,14},{8,0},{10,2},{12,4},{14,6},{1,9},{3,11}... | collective-permute-start | bytes 983048 | tf_op jit(solution)/shard_map/ppermute | solution.py:23
  16.4 135.0 %collective-permute-start.12 = (bf16[1,1,40,4096]{3,2,1,0:T(8,128)(2,1)}, bf16[1,1,40,4096]{3,2,1,0:T(8,128)(2,1)}, u32[]{:S(2)}, u32[]{:S(2)}) collective-permute-start(bf16[1,1,40,4096]{3,2,1,0:T(8,128)(2,1)} %shard_map.107), channel_id=1, source_target_pairs={{0,8},{2,10},{4,12},{6,14},{8,0},{10,2},{12,4},{14,6},{1,9},{3,11}... | collective-permute-start | bytes 983048 | tf_op jit(solution)/shard_map/ppermute | solution.py:23
  19.1 134.7 %collective-permute-start.11 = (bf16[1,1,40,4096]{3,2,1,0:T(8,128)(2,1)}, bf16[1,1,40,4096]{3,2,1,0:T(8,128)(2,1)}, u32[]{:S(2)}, u32[]{:S(2)}) collective-permute-start(bf16[1,1,40,4096]{3,2,1,0:T(8,128)(2,1)} %shard_map.106), channel_id=1, source_target_pairs={{0,8},{2,10},{4,12},{6,14},{8,0},{10,2},{12,4},{14,6},{1,9},{3,11}... | collective-permute-start | bytes 983048 | tf_op jit(solution)/shard_map/ppermute | solution.py:23
  29.6 7.5 %copy-start.8 = (s32[4]{0:T(128)S(1)}, s32[4]{0:T(128)}, u32[]{:S(2)}) copy-start(s32[4]{0:T(128)} %param.14) | copy-start | bytes 52
  30.3 53.2 %all-to-all-start = ((f32[16,4,1280]{2,1,0:T(4,128)}), f32[16,4,1280]{2,1,0:T(4,128)S(1)}, u32[]{:S(2)}, u32[]{:S(2)}) async-start(f32[16,4,1280]{2,1,0:T(4,128)} %broadcast_in_dim.104), calls=%async_computation | async-start | bytes 655360 | tf_op jit(solution)/shard_map/all_to_all | solution.py:150
  49.0 61.3 %copy-start.1 = (bf16[1,1,40,4096]{3,2,1,0:T(8,128)(2,1)S(1)}, bf16[1,1,40,4096]{3,2,1,0:T(8,128)(2,1)}, u32[]{:S(2)}) copy-start(bf16[1,1,40,4096]{3,2,1,0:T(8,128)(2,1)} %shard_map.105) | copy-start | bytes 983044
  88.5 14.5 %all-to-all-start.1 = ((f32[16,16,256]{2,1,0:T(8,128)}), f32[16,16,256]{2,1,0:T(8,128)S(1)}, u32[]{:S(2)}, u32[]{:S(2)}) async-start(f32[16,16,256]{2,1,0:T(8,128)} %copy.115), calls=%async_computation.1 | async-start | bytes 524288 | tf_op jit(solution)/shard_map/all_to_all | solution.py:150
  110.3 15.8 %copy-start.4 = (bf16[1,1,40,4096]{3,2,1,0:T(8,128)(2,1)}, bf16[1,1,40,4096]{3,2,1,0:T(8,128)(2,1)S(1)}, u32[]{:S(2)}) copy-start(bf16[1,1,40,4096]{3,2,1,0:T(8,128)(2,1)S(1)} %collective-permute-done.15.data_ref) | copy-start | bytes 983044
  110.3 44.0 %collective-permute-start.10 = (bf16[1,1,40,4096]{3,2,1,0:T(8,128)(2,1)S(1)}, bf16[1,1,40,4096]{3,2,1,0:T(8,128)(2,1)}, u32[]{:S(2)}, u32[]{:S(2)}) collective-permute-start(bf16[1,1,40,4096]{3,2,1,0:T(8,128)(2,1)S(1)} %copy-done.1), channel_id=1, source_target_pairs={{0,8},{2,10},{4,12},{6,14},{8,0},{10,2},{12,4},{14,6},{1,9},{3,11}... | collective-permute-start | bytes 983048 | tf_op jit(solution)/shard_map/ppermute | solution.py:23
  118.8 38.0 %all-to-all-start.2 = ((f32[16,4,512]{2,1,0:T(4,128)}), f32[16,4,512]{2,1,0:T(4,128)S(1)}, u32[]{:S(2)}, u32[]{:S(2)}) async-start(f32[16,4,512]{2,1,0:T(4,128)} %convolution_bitcast_fusion), calls=%async_computation.2 | async-start | bytes 262144 | tf_op jit(solution)/shard_map/all_to_all | solution.py:150
  142.8 79.6 %copy-start.3 = (bf16[1,1,40,4096]{3,2,1,0:T(8,128)(2,1)S(1)}, bf16[1,1,40,4096]{3,2,1,0:T(8,128)(2,1)}, u32[]{:S(2)}) copy-start(bf16[1,1,40,4096]{3,2,1,0:T(8,128)(2,1)} %shard_map.97) | copy-start | bytes 983044
  145.4 91.1 %copy-start.2 = (bf16[1,1,40,4096]{3,2,1,0:T(8,128)(2,1)S(1)}, bf16[1,1,40,4096]{3,2,1,0:T(8,128)(2,1)}, u32[]{:S(2)}) copy-start(bf16[1,1,40,4096]{3,2,1,0:T(8,128)(2,1)} %shard_map.96) | copy-start | bytes 983044
  148.4 45.9 %collective-permute-start.9 = (bf16[1,1,40,4096]{3,2,1,0:T(8,128)(2,1)}, bf16[1,1,40,4096]{3,2,1,0:T(8,128)(2,1)}, u32[]{:S(2)}, u32[]{:S(2)}) collective-permute-start(bf16[1,1,40,4096]{3,2,1,0:T(8,128)(2,1)} %shard_map.104), channel_id=1, source_target_pairs={{0,8},{2,10},{4,12},{6,14},{8,0},{10,2},{12,4},{14,6},{1,9},{3,11}... | collective-permute-start | bytes 983048 | tf_op jit(solution)/shard_map/ppermute | solution.py:23
  150.9 57.5 %collective-permute-start.8 = (bf16[1,1,40,4096]{3,2,1,0:T(8,128)(2,1)}, bf16[1,1,40,4096]{3,2,1,0:T(8,128)(2,1)}, u32[]{:S(2)}, u32[]{:S(2)}) collective-permute-start(bf16[1,1,40,4096]{3,2,1,0:T(8,128)(2,1)} %shard_map.103), channel_id=1, source_target_pairs={{0,8},{2,10},{4,12},{6,14},{8,0},{10,2},{12,4},{14,6},{1,9},{3,11}... | collective-permute-start | bytes 983048 | tf_op jit(solution)/shard_map/ppermute | solution.py:23
  151.4 71.0 %collective-permute-start.7 = (bf16[1,1,40,4096]{3,2,1,0:T(8,128)(2,1)}, bf16[1,1,40,4096]{3,2,1,0:T(8,128)(2,1)}, u32[]{:S(2)}, u32[]{:S(2)}) collective-permute-start(bf16[1,1,40,4096]{3,2,1,0:T(8,128)(2,1)} %shard_map.102), channel_id=1, source_target_pairs={{0,8},{2,10},{4,12},{6,14},{8,0},{10,2},{12,4},{14,6},{1,9},{3,11}... | collective-permute-start | bytes 983048 | tf_op jit(solution)/shard_map/ppermute | solution.py:23
  153.9 82.6 %collective-permute-start.6 = (bf16[1,1,40,4096]{3,2,1,0:T(8,128)(2,1)}, bf16[1,1,40,4096]{3,2,1,0:T(8,128)(2,1)}, u32[]{:S(2)}, u32[]{:S(2)}) collective-permute-start(bf16[1,1,40,4096]{3,2,1,0:T(8,128)(2,1)} %shard_map.101), channel_id=1, source_target_pairs={{0,8},{2,10},{4,12},{6,14},{8,0},{10,2},{12,4},{14,6},{1,9},{3,11}... | collective-permute-start | bytes 983048 | tf_op jit(solution)/shard_map/ppermute | solution.py:23
  154.4 96.2 %collective-permute-start.5 = (bf16[1,1,40,4096]{3,2,1,0:T(8,128)(2,1)}, bf16[1,1,40,4096]{3,2,1,0:T(8,128)(2,1)S(1)}, u32[]{:S(2)}, u32[]{:S(2)}) collective-permute-start(bf16[1,1,40,4096]{3,2,1,0:T(8,128)(2,1)} %shard_map.100), channel_id=1, source_target_pairs={{0,8},{2,10},{4,12},{6,14},{8,0},{10,2},{12,4},{14,6},{1,9},{3,11}... | collective-permute-start | bytes 983048 | tf_op jit(solution)/shard_map/ppermute | solution.py:23
  157.5 151.6 %all-to-all-start.3 = ((bf16[16,4,512]{2,1,0:T(4,128)(2,1)}), bf16[16,4,512]{2,1,0:T(4,128)(2,1)S(1)}, u32[]{:S(2)}, u32[]{:S(2)}) async-start(bf16[16,4,512]{2,1,0:T(4,128)(2,1)} %broadcast_in_dim.113), calls=%async_computation.3 | async-start | bytes 131072 | tf_op jit(solution)/shard_map/all_to_all | solution.py:150
  194.4 102.6 %collective-permute-start.4 = (bf16[1,1,40,4096]{3,2,1,0:T(8,128)(2,1)}, bf16[1,1,40,4096]{3,2,1,0:T(8,128)(2,1)}, u32[]{:S(2)}, u32[]{:S(2)}) collective-permute-start(bf16[1,1,40,4096]{3,2,1,0:T(8,128)(2,1)} %shard_map.99), channel_id=1, source_target_pairs={{0,8},{2,10},{4,12},{6,14},{8,0},{10,2},{12,4},{14,6},{1,9},{3,11}... | collective-permute-start | bytes 983048 | tf_op jit(solution)/shard_map/ppermute | solution.py:23
  208.4 91.0 %collective-permute-start.3 = (bf16[1,1,40,4096]{3,2,1,0:T(8,128)(2,1)}, bf16[1,1,40,4096]{3,2,1,0:T(8,128)(2,1)}, u32[]{:S(2)}, u32[]{:S(2)}) collective-permute-start(bf16[1,1,40,4096]{3,2,1,0:T(8,128)(2,1)} %shard_map.98), channel_id=1, source_target_pairs={{0,8},{2,10},{4,12},{6,14},{8,0},{10,2},{12,4},{14,6},{1,9},{3,11}... | collective-permute-start | bytes 983048 | tf_op jit(solution)/shard_map/ppermute | solution.py:23
  222.4 79.4 %collective-permute-start.2 = (bf16[1,1,40,4096]{3,2,1,0:T(8,128)(2,1)S(1)}, bf16[1,1,40,4096]{3,2,1,0:T(8,128)(2,1)}, u32[]{:S(2)}, u32[]{:S(2)}) collective-permute-start(bf16[1,1,40,4096]{3,2,1,0:T(8,128)(2,1)S(1)} %copy-done.3), channel_id=1, source_target_pairs={{0,8},{2,10},{4,12},{6,14},{8,0},{10,2},{12,4},{14,6},{1,9},{3,11}... | collective-permute-start | bytes 983048 | tf_op jit(solution)/shard_map/ppermute | solution.py:23
  236.5 67.8 %collective-permute-start.1 = (bf16[1,1,40,4096]{3,2,1,0:T(8,128)(2,1)S(1)}, bf16[1,1,40,4096]{3,2,1,0:T(8,128)(2,1)}, u32[]{:S(2)}, u32[]{:S(2)}) collective-permute-start(bf16[1,1,40,4096]{3,2,1,0:T(8,128)(2,1)S(1)} %copy-done.2), channel_id=1, source_target_pairs={{0,8},{2,10},{4,12},{6,14},{8,0},{10,2},{12,4},{14,6},{1,9},{3,11}... | collective-permute-start | bytes 983048 | tf_op jit(solution)/shard_map/ppermute | solution.py:23
  250.5 19.7 %copy-start.5 = (bf16[1,1,40,4096]{3,2,1,0:T(8,128)(2,1)}, bf16[1,1,40,4096]{3,2,1,0:T(8,128)(2,1)S(1)}, u32[]{:S(2)}) copy-start(bf16[1,1,40,4096]{3,2,1,0:T(8,128)(2,1)S(1)} %collective-permute-done.5.data_ref) | copy-start | bytes 983044
  250.5 56.1 %collective-permute-start = (bf16[1,1,40,4096]{3,2,1,0:T(8,128)(2,1)}, bf16[1,1,40,4096]{3,2,1,0:T(8,128)(2,1)}, u32[]{:S(2)}, u32[]{:S(2)}) collective-permute-start(bf16[1,1,40,4096]{3,2,1,0:T(8,128)(2,1)} %shard_map.95), channel_id=1, source_target_pairs={{0,8},{2,10},{4,12},{6,14},{8,0},{10,2},{12,4},{14,6},{1,9},{3,11}... | collective-permute-start | bytes 983048 | tf_op jit(solution)/shard_map/ppermute | solution.py:23

commit v2 on v1

--- a/solution.py
+++ b/solution.py
@@ -14,7 +14,7 @@
 RANKS = 8
 ROW_BLOCKS = 16
 CHUNKS = 16
-WAVE_STARTS = (0, 2, 5, 8, 11)
+WAVE_STARTS = (0, 2, 6, 10, 13)
 
 
 def passed_along(value, axis, steps):
@@ -62,6 +62,19 @@
             flops=0, bytes_accessed=4 * rows * weight.shape[3], transcendentals=0
         ),
     )(targets, weight)
+
+
+def joined(shares):
+    count, seq_count, share = shares.shape
+
+    def kernel(share_ref, out_ref):
+        for index in range(count):
+            out_ref[:, index * share : (index + 1) * share] = share_ref[index]
+
+    return pl.pallas_call(
+        kernel,
+        out_shape=jax.ShapeDtypeStruct((seq_count, count * share), shares.dtype),
+    )(shares)
 
 
 def placed_blocks(slots, data, dest, full_shape, offset, per, rows, first_row):
@@ -251,7 +264,7 @@
     own_out = (own_hidden.astype(jnp.float32) + jnp.sum(shares_in, 0)).astype(jnp.bfloat16)
     send_wave(4)
     all_out = exchanged(jnp.broadcast_to(own_out[None], (device_count,) + own_out.shape))
-    mixed_out = jnp.transpose(all_out, (1, 0, 2)).reshape(seq_count, width)
+    mixed_out = joined(all_out)
 
     full_shape = (1, 1, cols_dev, ROW_BLOCKS * block_rows)
     sources = (own_section - jnp.arange(section_count, dtype=jnp.int32)) % section_count

time: 312 us -> 314 us (level)
  no operation moved by 1% of the time
where the time goes in v2:
time: 314 us; the launch traced here: 311 us
  waiting for transfers between devices  116 us (37%)
  Pallas kernels  94.5 us (30%)
  starting transfers between devices  56 us (18%)
  local copies, waits for them, and re-layouts  20.9 us (7%)
  matrix products  15.9 us (5%)
  other arithmetic  7.26 us (2%)
    ppermute x16, waiting for transfers between devices, passed_along(): return lax.ppermute(value, axis, pairs)  75.3 us
    pallas_call x17, Pallas kernels, placed_blocks(): pl.pallas_call(kernel, out_shape=jax.ShapeDtypeStruct(full_shape, data.dt...  54.4 us
    all_to_all x4, waiting for transfers between devices, exchanged(): lax.all_to_all(blocks, ('tp', 'sub'), split_axis=0, concat_axis=0, tiled=...  40.3 us
    pallas_call x16, Pallas kernels, cut_rows(): pl.pallas_call(kernel, out_shape=jax.ShapeDtypeStruct(shape, weight.dtype...  38.6 us
    ppermute x16, starting transfers between devices, passed_along(): return lax.ppermute(value, axis, pairs)  35.7 us
    all_to_all x4, starting transfers between devices, exchanged(): lax.all_to_all(blocks, ('tp', 'sub'), split_axis=0, concat_axis=0, tiled=...  20.3 us
    dot_general x1, local copies, waits for them, and re-layouts, shards(): partial_out = jnp.dot(attended, wo, preferred_element_type=jnp.float32)  11.9 us
    dot_general x1, matrix products, shards(): lax.dot_general(own_rows.reshape(seq_count, rows_old), wqkv_old[0, 0], ((...  6.78 us
  transfers between devices with their start and end apart: 20, of which 7 were waited for; matrix products, arithmetic and copies ran while one was open for 14% of the time, Pallas kernels for 29%

profile of v2, /device:TPU:8, one launch (start us, length us, event | category | flops | bytes accessed | tf_op | source)
XLA Modules:
  0.0 311.3 jit_solution(10607168741516046210)
XLA Ops:
  1.2 2.5 shard_map.111
  3.7 2.6 collective-permute-start.15
  11.4 2.6 collective-permute-start.13
  19.1 2.6 collective-permute-start.11
  22.8 6.8 %fusion = f32[4,1280]{1,0:T(4,128)S(1)} fusion(bf16[4,4096]{1,0:T(4,128)(2,1)S(1)} %bitcast.113, bf16[1,1,1280,4096]{3,2,1,0:T(8,128)(2,1)} %data_ref.1), kind=kOutput, calls=%fused_computation.4 | convolution fusion | flops 41943040 | bytes 10539008 | tf_op jit(solution)/shard_map/dot_general | solution.py:170
  30.3 4.3 %all-to-all-start = ((f32[16,4,1280]{2,1,0:T(4,128)}), f32[16,4,1280]{2,1,0:T(4,128)S(1)}, u32[]{:S(2)}, u32[]{:S(2)}) async-start(f32[16,4,1280]{2,1,0:T(4,128)} %broadcast_in_dim.104), calls=%async_computation | async-start | bytes 655360 | tf_op jit(solution)/shard_map/all_to_all | solution.py:163
  37.1 11.9 %copy.126 = bf16[8192,512]{1,0:T(8,128)(2,1)} copy(bf16[8192,512]{0,1:T(8,128)(2,1)} %bitcast.101) | data formatting | bytes 16777216 | tf_op jit(solution)/shard_map/dot_general | solution.py:258
  49.2 34.4 %all-to-all-done = f32[16,4,1280]{2,1,0:T(4,128)S(1)} async-done(((f32[16,4,1280]{2,1,0:T(4,128)}), f32[16,4,1280]{2,1,0:T(4,128)S(1)}, u32[]{:S(2)}, u32[]{:S(2)}) %all-to-all-start) | async-done | bytes 327712 | tf_op jit(solution)/shard_map/all_to_all | solution.py:163
  88.5 6.9 %all-to-all-start.1 = ((f32[16,16,256]{2,1,0:T(8,128)}), f32[16,16,256]{2,1,0:T(8,128)S(1)}, u32[]{:S(2)}, u32[]{:S(2)}) async-start(f32[16,16,256]{2,1,0:T(8,128)} %copy.115), calls=%async_computation.1 | async-start | bytes 524288 | tf_op jit(solution)/shard_map/all_to_all | solution.py:163
  97.0 6.0 %all-to-all-done.1 = f32[16,16,256]{2,1,0:T(8,128)S(1)} async-done(((f32[16,16,256]{2,1,0:T(8,128)}), f32[16,16,256]{2,1,0:T(8,128)S(1)}, u32[]{:S(2)}, u32[]{:S(2)}) %all-to-all-start.1) | async-done | bytes 262176 | tf_op jit(solution)/shard_map/all_to_all | solution.py:163
  103.0 2.5 copy.116
  112.5 6.3 %convolution_bitcast_fusion = f32[16,4,512]{2,1,0:T(4,128)} fusion(bf16[16,512,512]{2,1,0:T(8,128)(2,1)} %bitcast.100, f32[4,4,128]{2,1,0:T(4,128)S(1)} %gather_fusion.2, f32[4,4,128]{2,0,1:T(4,128)S(1)} %copy.120, f32[4,4]{0,1:T(4,128)S(1)} %copy.122, f32[4,4]{0,1:T(4,128)S(1)} %copy.121, f32[4,4]{0,1:T(4,128)S(1)} %copy.119, ...), kind=kOutput, calls=%fused_computation.13 | convolution fusion | flops 33566720 | bytes 8536260 | tf_op jit(solution)/shard_map/dot_general | solution.py:258
  118.8 4.9 %all-to-all-start.2 = ((f32[16,4,512]{2,1,0:T(4,128)}), f32[16,4,512]{2,1,0:T(4,128)S(1)}, u32[]{:S(2)}, u32[]{:S(2)}) async-start(f32[16,4,512]{2,1,0:T(4,128)} %convolution_bitcast_fusion), calls=%async_computation.2 | async-start | bytes 262144 | tf_op jit(solution)/shard_map/all_to_all | solution.py:163
  142.9 2.5 shard_map.97
  145.4 2.5 shard_map.96
  148.5 2.5 collective-permute-start.9
  157.6 4.2 %all-to-all-start.3 = ((bf16[16,4,512]{2,1,0:T(4,128)(2,1)}), bf16[16,4,512]{2,1,0:T(4,128)(2,1)S(1)}, u32[]{:S(2)}, u32[]{:S(2)}) async-start(bf16[16,4,512]{2,1,0:T(4,128)(2,1)} %broadcast_in_dim.113), calls=%async_computation.3 | async-start | bytes 131072 | tf_op jit(solution)/shard_map/all_to_all | solution.py:163
  161.8 32.6 %collective-permute-done.9.data_ref = bf16[1,1,40,4096]{3,2,1,0:T(8,128)(2,1)} collective-permute-done((bf16[1,1,40,4096]{3,2,1,0:T(8,128)(2,1)}, bf16[1,1,40,4096]{3,2,1,0:T(8,128)(2,1)}, u32[]{:S(2)}, u32[]{:S(2)}) %collective-permute-start.9) | collective-permute-done | bytes 327712 | tf_op jit(solution)/shard_map/ppermute | solution.py:23
  194.4 3.4 %collective-permute-start.4 = (bf16[1,1,40,4096]{3,2,1,0:T(8,128)(2,1)}, bf16[1,1,40,4096]{3,2,1,0:T(8,128)(2,1)}, u32[]{:S(2)}, u32[]{:S(2)}) collective-permute-start(bf16[1,1,40,4096]{3,2,1,0:T(8,128)(2,1)} %shard_map.100), channel_id=1, source_target_pairs={{0,8},{2,10},{4,12},{6,14},{8,0},{10,2},{12,4},{14,6},{1,9},{3,11}... | collective-permute-start | bytes 983048 | tf_op jit(solution)/shard_map/ppermute | solution.py:23
  197.8 10.7 %collective-permute-done.8.data_ref = bf16[1,1,40,4096]{3,2,1,0:T(8,128)(2,1)} collective-permute-done((bf16[1,1,40,4096]{3,2,1,0:T(8,128)(2,1)}, bf16[1,1,40,4096]{3,2,1,0:T(8,128)(2,1)}, u32[]{:S(2)}, u32[]{:S(2)}) %collective-permute-start.8) | collective-permute-done | bytes 327712 | tf_op jit(solution)/shard_map/ppermute | solution.py:23
  208.4 3.4 %collective-permute-start.3 = (bf16[1,1,40,4096]{3,2,1,0:T(8,128)(2,1)}, bf16[1,1,40,4096]{3,2,1,0:T(8,128)(2,1)}, u32[]{:S(2)}, u32[]{:S(2)}) collective-permute-start(bf16[1,1,40,4096]{3,2,1,0:T(8,128)(2,1)} %shard_map.99), channel_id=1, source_target_pairs={{0,8},{2,10},{4,12},{6,14},{8,0},{10,2},{12,4},{14,6},{1,9},{3,11}... | collective-permute-start | bytes 983048 | tf_op jit(solution)/shard_map/ppermute | solution.py:23
  211.8 10.7 %collective-permute-done.7.data_ref = bf16[1,1,40,4096]{3,2,1,0:T(8,128)(2,1)} collective-permute-done((bf16[1,1,40,4096]{3,2,1,0:T(8,128)(2,1)}, bf16[1,1,40,4096]{3,2,1,0:T(8,128)(2,1)}, u32[]{:S(2)}, u32[]{:S(2)}) %collective-permute-start.7) | collective-permute-done | bytes 327712 | tf_op jit(solution)/shard_map/ppermute | solution.py:23
  222.5 3.4 %collective-permute-start.2 = (bf16[1,1,40,4096]{3,2,1,0:T(8,128)(2,1)S(1)}, bf16[1,1,40,4096]{3,2,1,0:T(8,128)(2,1)}, u32[]{:S(2)}, u32[]{:S(2)}) collective-permute-start(bf16[1,1,40,4096]{3,2,1,0:T(8,128)(2,1)S(1)} %copy-done.3), channel_id=1, source_target_pairs={{0,8},{2,10},{4,12},{6,14},{8,0},{10,2},{12,4},{14,6},{1,9},{3,11}... | collective-permute-start | bytes 983048 | tf_op jit(solution)/shard_map/ppermute | solution.py:23
  225.9 10.7 %collective-permute-done.6.data_ref = bf16[1,1,40,4096]{3,2,1,0:T(8,128)(2,1)} collective-permute-done((bf16[1,1,40,4096]{3,2,1,0:T(8,128)(2,1)}, bf16[1,1,40,4096]{3,2,1,0:T(8,128)(2,1)}, u32[]{:S(2)}, u32[]{:S(2)}) %collective-permute-start.6) | collective-permute-done | bytes 327712 | tf_op jit(solution)/shard_map/ppermute | solution.py:23
  236.5 3.4 %collective-permute-start.1 = (bf16[1,1,40,4096]{3,2,1,0:T(8,128)(2,1)S(1)}, bf16[1,1,40,4096]{3,2,1,0:T(8,128)(2,1)}, u32[]{:S(2)}, u32[]{:S(2)}) collective-permute-start(bf16[1,1,40,4096]{3,2,1,0:T(8,128)(2,1)S(1)} %copy-done.2), channel_id=1, source_target_pairs={{0,8},{2,10},{4,12},{6,14},{8,0},{10,2},{12,4},{14,6},{1,9},{3,11}... | collective-permute-start | bytes 983048 | tf_op jit(solution)/shard_map/ppermute | solution.py:23
  239.9 10.7 %collective-permute-done.5.data_ref = bf16[1,1,40,4096]{3,2,1,0:T(8,128)(2,1)S(1)} collective-permute-done((bf16[1,1,40,4096]{3,2,1,0:T(8,128)(2,1)}, bf16[1,1,40,4096]{3,2,1,0:T(8,128)(2,1)S(1)}, u32[]{:S(2)}, u32[]{:S(2)}) %collective-permute-start.5) | collective-permute-done | bytes 327712 | tf_op jit(solution)/shard_map/ppermute | solution.py:23
  250.6 3.3 %collective-permute-start = (bf16[1,1,40,4096]{3,2,1,0:T(8,128)(2,1)}, bf16[1,1,40,4096]{3,2,1,0:T(8,128)(2,1)}, u32[]{:S(2)}, u32[]{:S(2)}) collective-permute-start(bf16[1,1,40,4096]{3,2,1,0:T(8,128)(2,1)} %shard_map.96), channel_id=1, source_target_pairs={{0,8},{2,10},{4,12},{6,14},{8,0},{10,2},{12,4},{14,6},{1,9},{3,11}... | collective-permute-start | bytes 983048 | tf_op jit(solution)/shard_map/ppermute | solution.py:23
  254.6 15.7 %shard_map.112.rest_0_ = bf16[1,1,640,8192]{3,2,1,0:T(8,128)(2,1)} custom-call(s32[17]{0:T(128)} %pad_add_fusion.slot_ref, bf16[1,1,1280,4096]{3,2,1,0:T(8,128)(2,1)} %data_ref.1), custom_call_target="tpu_custom_call" | custom-call | bytes 10485760 | tf_op jit(solution)/shard_map/pallas_call | solution.py:117
  277.6 2.4 shard_map.116.rest_0_
  280.0 2.4 shard_map.117.rest_0_
  282.4 2.4 shard_map.118.rest_0_
  292.1 2.4 shard_map.122.rest_0_
  (130 shorter events, 86.8 us)
Async XLA Ops:
  0.6 83.3 %copy-start = (bf16[4,256,1024]{2,1,0:T(8,128)(2,1)S(1)}, bf16[4,256,1024]{2,1,0:T(8,128)(2,1)}, u32[]{:S(2)}) copy-start(bf16[4,256,1024]{2,1,0:T(8,128)(2,1)} %param.12) | copy-start | bytes 6291460
  3.7 106.6 %collective-permute-start.15 = (bf16[1,1,40,4096]{3,2,1,0:T(8,128)(2,1)}, bf16[1,1,40,4096]{3,2,1,0:T(8,128)(2,1)S(1)}, u32[]{:S(2)}, u32[]{:S(2)}) collective-permute-start(bf16[1,1,40,4096]{3,2,1,0:T(8,128)(2,1)} %shard_map.111), channel_id=1, source_target_pairs={{0,8},{2,10},{4,12},{6,14},{8,0},{10,2},{12,4},{14,6},{1,9},{3,11}... | collective-permute-start | bytes 983048 | tf_op jit(solution)/shard_map/ppermute | solution.py:23
  8.7 139.8 %collective-permute-start.14 = (bf16[1,1,40,4096]{3,2,1,0:T(8,128)(2,1)}, bf16[1,1,40,4096]{3,2,1,0:T(8,128)(2,1)}, u32[]{:S(2)}, u32[]{:S(2)}) collective-permute-start(bf16[1,1,40,4096]{3,2,1,0:T(8,128)(2,1)} %shard_map.110), channel_id=1, source_target_pairs={{0,8},{2,10},{4,12},{6,14},{8,0},{10,2},{12,4},{14,6},{1,9},{3,11}... | collective-permute-start | bytes 983048 | tf_op jit(solution)/shard_map/ppermute | solution.py:23
  11.4 10.3 %copy-start.10 = (s32[16]{0:T(128)S(1)}, s32[16]{0:T(128)}, u32[]{:S(2)}) copy-start(s32[16]{0:T(128)} %param.15) | copy-start | bytes 196
  11.4 10.4 %copy-start.6 = (bf16[4,8192]{1,0:T(4,128)(2,1)S(1)}, bf16[4,8192]{1,0:T(4,128)(2,1)}, u32[]{:S(2)}) copy-start(bf16[4,8192]{1,0:T(4,128)(2,1)} %param.8) | copy-start | bytes 196612
  11.4 10.6 %copy-start.8 = (f32[8192]{0:T(1024)S(1)}, f32[8192]{0:T(1024)}, u32[]{:S(2)}) copy-start(f32[8192]{0:T(1024)} %param.9) | copy-start | bytes 98308
  11.4 139.5 %collective-permute-start.13 = (bf16[1,1,40,4096]{3,2,1,0:T(8,128)(2,1)}, bf16[1,1,40,4096]{3,2,1,0:T(8,128)(2,1)}, u32[]{:S(2)}, u32[]{:S(2)}) collective-permute-start(bf16[1,1,40,4096]{3,2,1,0:T(8,128)(2,1)} %shard_map.109), channel_id=1, source_target_pairs={{0,8},{2,10},{4,12},{6,14},{8,0},{10,2},{12,4},{14,6},{1,9},{3,11}... | collective-permute-start | bytes 983048 | tf_op jit(solution)/shard_map/ppermute | solution.py:23
  16.4 135.1 %collective-permute-start.12 = (bf16[1,1,40,4096]{3,2,1,0:T(8,128)(2,1)}, bf16[1,1,40,4096]{3,2,1,0:T(8,128)(2,1)}, u32[]{:S(2)}, u32[]{:S(2)}) collective-permute-start(bf16[1,1,40,4096]{3,2,1,0:T(8,128)(2,1)} %shard_map.108), channel_id=1, source_target_pairs={{0,8},{2,10},{4,12},{6,14},{8,0},{10,2},{12,4},{14,6},{1,9},{3,11}... | collective-permute-start | bytes 983048 | tf_op jit(solution)/shard_map/ppermute | solution.py:23
  19.1 134.8 %collective-permute-start.11 = (bf16[1,1,40,4096]{3,2,1,0:T(8,128)(2,1)}, bf16[1,1,40,4096]{3,2,1,0:T(8,128)(2,1)}, u32[]{:S(2)}, u32[]{:S(2)}) collective-permute-start(bf16[1,1,40,4096]{3,2,1,0:T(8,128)(2,1)} %shard_map.107), channel_id=1, source_target_pairs={{0,8},{2,10},{4,12},{6,14},{8,0},{10,2},{12,4},{14,6},{1,9},{3,11}... | collective-permute-start | bytes 983048 | tf_op jit(solution)/shard_map/ppermute | solution.py:23
  29.6 7.5 %copy-start.9 = (s32[4]{0:T(128)S(1)}, s32[4]{0:T(128)}, u32[]{:S(2)}) copy-start(s32[4]{0:T(128)} %param.14) | copy-start | bytes 52
  30.3 53.2 %all-to-all-start = ((f32[16,4,1280]{2,1,0:T(4,128)}), f32[16,4,1280]{2,1,0:T(4,128)S(1)}, u32[]{:S(2)}, u32[]{:S(2)}) async-start(f32[16,4,1280]{2,1,0:T(4,128)} %broadcast_in_dim.104), calls=%async_computation | async-start | bytes 655360 | tf_op jit(solution)/shard_map/all_to_all | solution.py:163
  49.0 61.3 %copy-start.1 = (bf16[1,1,40,4096]{3,2,1,0:T(8,128)(2,1)S(1)}, bf16[1,1,40,4096]{3,2,1,0:T(8,128)(2,1)}, u32[]{:S(2)}) copy-start(bf16[1,1,40,4096]{3,2,1,0:T(8,128)(2,1)} %shard_map.106) | copy-start | bytes 983044
  88.5 14.5 %all-to-all-start.1 = ((f32[16,16,256]{2,1,0:T(8,128)}), f32[16,16,256]{2,1,0:T(8,128)S(1)}, u32[]{:S(2)}, u32[]{:S(2)}) async-start(f32[16,16,256]{2,1,0:T(8,128)} %copy.115), calls=%async_computation.1 | async-start | bytes 524288 | tf_op jit(solution)/shard_map/all_to_all | solution.py:163
  110.3 15.8 %copy-start.4 = (bf16[1,1,40,4096]{3,2,1,0:T(8,128)(2,1)}, bf16[1,1,40,4096]{3,2,1,0:T(8,128)(2,1)S(1)}, u32[]{:S(2)}) copy-start(bf16[1,1,40,4096]{3,2,1,0:T(8,128)(2,1)S(1)} %collective-permute-done.15.data_ref) | copy-start | bytes 983044
  110.3 44.1 %collective-permute-start.10 = (bf16[1,1,40,4096]{3,2,1,0:T(8,128)(2,1)S(1)}, bf16[1,1,40,4096]{3,2,1,0:T(8,128)(2,1)}, u32[]{:S(2)}, u32[]{:S(2)}) collective-permute-start(bf16[1,1,40,4096]{3,2,1,0:T(8,128)(2,1)S(1)} %copy-done.1), channel_id=1, source_target_pairs={{0,8},{2,10},{4,12},{6,14},{8,0},{10,2},{12,4},{14,6},{1,9},{3,11}... | collective-permute-start | bytes 983048 | tf_op jit(solution)/shard_map/ppermute | solution.py:23
  118.8 38.1 %all-to-all-start.2 = ((f32[16,4,512]{2,1,0:T(4,128)}), f32[16,4,512]{2,1,0:T(4,128)S(1)}, u32[]{:S(2)}, u32[]{:S(2)}) async-start(f32[16,4,512]{2,1,0:T(4,128)} %convolution_bitcast_fusion), calls=%async_computation.2 | async-start | bytes 262144 | tf_op jit(solution)/shard_map/all_to_all | solution.py:163
  142.9 79.6 %copy-start.3 = (bf16[1,1,40,4096]{3,2,1,0:T(8,128)(2,1)S(1)}, bf16[1,1,40,4096]{3,2,1,0:T(8,128)(2,1)}, u32[]{:S(2)}) copy-start(bf16[1,1,40,4096]{3,2,1,0:T(8,128)(2,1)} %shard_map.98) | copy-start | bytes 983044
  145.4 91.1 %copy-start.2 = (bf16[1,1,40,4096]{3,2,1,0:T(8,128)(2,1)S(1)}, bf16[1,1,40,4096]{3,2,1,0:T(8,128)(2,1)}, u32[]{:S(2)}) copy-start(bf16[1,1,40,4096]{3,2,1,0:T(8,128)(2,1)} %shard_map.97) | copy-start | bytes 983044
  148.5 45.9 %collective-permute-start.9 = (bf16[1,1,40,4096]{3,2,1,0:T(8,128)(2,1)}, bf16[1,1,40,4096]{3,2,1,0:T(8,128)(2,1)}, u32[]{:S(2)}, u32[]{:S(2)}) collective-permute-start(bf16[1,1,40,4096]{3,2,1,0:T(8,128)(2,1)} %shard_map.105), channel_id=1, source_target_pairs={{0,8},{2,10},{4,12},{6,14},{8,0},{10,2},{12,4},{14,6},{1,9},{3,11}... | collective-permute-start | bytes 983048 | tf_op jit(solution)/shard_map/ppermute | solution.py:23
  151.0 57.5 %collective-permute-start.8 = (bf16[1,1,40,4096]{3,2,1,0:T(8,128)(2,1)}, bf16[1,1,40,4096]{3,2,1,0:T(8,128)(2,1)}, u32[]{:S(2)}, u32[]{:S(2)}) collective-permute-start(bf16[1,1,40,4096]{3,2,1,0:T(8,128)(2,1)} %shard_map.104), channel_id=1, source_target_pairs={{0,8},{2,10},{4,12},{6,14},{8,0},{10,2},{12,4},{14,6},{1,9},{3,11}... | collective-permute-start | bytes 983048 | tf_op jit(solution)/shard_map/ppermute | solution.py:23
  151.5 71.0 %collective-permute-start.7 = (bf16[1,1,40,4096]{3,2,1,0:T(8,128)(2,1)}, bf16[1,1,40,4096]{3,2,1,0:T(8,128)(2,1)}, u32[]{:S(2)}, u32[]{:S(2)}) collective-permute-start(bf16[1,1,40,4096]{3,2,1,0:T(8,128)(2,1)} %shard_map.103), channel_id=1, source_target_pairs={{0,8},{2,10},{4,12},{6,14},{8,0},{10,2},{12,4},{14,6},{1,9},{3,11}... | collective-permute-start | bytes 983048 | tf_op jit(solution)/shard_map/ppermute | solution.py:23
  153.9 82.6 %collective-permute-start.6 = (bf16[1,1,40,4096]{3,2,1,0:T(8,128)(2,1)}, bf16[1,1,40,4096]{3,2,1,0:T(8,128)(2,1)}, u32[]{:S(2)}, u32[]{:S(2)}) collective-permute-start(bf16[1,1,40,4096]{3,2,1,0:T(8,128)(2,1)} %shard_map.102), channel_id=1, source_target_pairs={{0,8},{2,10},{4,12},{6,14},{8,0},{10,2},{12,4},{14,6},{1,9},{3,11}... | collective-permute-start | bytes 983048 | tf_op jit(solution)/shard_map/ppermute | solution.py:23
  154.4 96.2 %collective-permute-start.5 = (bf16[1,1,40,4096]{3,2,1,0:T(8,128)(2,1)}, bf16[1,1,40,4096]{3,2,1,0:T(8,128)(2,1)S(1)}, u32[]{:S(2)}, u32[]{:S(2)}) collective-permute-start(bf16[1,1,40,4096]{3,2,1,0:T(8,128)(2,1)} %shard_map.101), channel_id=1, source_target_pairs={{0,8},{2,10},{4,12},{6,14},{8,0},{10,2},{12,4},{14,6},{1,9},{3,11}... | collective-permute-start | bytes 983048 | tf_op jit(solution)/shard_map/ppermute | solution.py:23
  157.6 151.6 %all-to-all-start.3 = ((bf16[16,4,512]{2,1,0:T(4,128)(2,1)}), bf16[16,4,512]{2,1,0:T(4,128)(2,1)S(1)}, u32[]{:S(2)}, u32[]{:S(2)}) async-start(bf16[16,4,512]{2,1,0:T(4,128)(2,1)} %broadcast_in_dim.113), calls=%async_computation.3 | async-start | bytes 131072 | tf_op jit(solution)/shard_map/all_to_all | solution.py:163
  194.4 102.6 %collective-permute-start.4 = (bf16[1,1,40,4096]{3,2,1,0:T(8,128)(2,1)}, bf16[1,1,40,4096]{3,2,1,0:T(8,128)(2,1)}, u32[]{:S(2)}, u32[]{:S(2)}) collective-permute-start(bf16[1,1,40,4096]{3,2,1,0:T(8,128)(2,1)} %shard_map.100), channel_id=1, source_target_pairs={{0,8},{2,10},{4,12},{6,14},{8,0},{10,2},{12,4},{14,6},{1,9},{3,11}... | collective-permute-start | bytes 983048 | tf_op jit(solution)/shard_map/ppermute | solution.py:23
  208.4 91.0 %collective-permute-start.3 = (bf16[1,1,40,4096]{3,2,1,0:T(8,128)(2,1)}, bf16[1,1,40,4096]{3,2,1,0:T(8,128)(2,1)}, u32[]{:S(2)}, u32[]{:S(2)}) collective-permute-start(bf16[1,1,40,4096]{3,2,1,0:T(8,128)(2,1)} %shard_map.99), channel_id=1, source_target_pairs={{0,8},{2,10},{4,12},{6,14},{8,0},{10,2},{12,4},{14,6},{1,9},{3,11}... | collective-permute-start | bytes 983048 | tf_op jit(solution)/shard_map/ppermute | solution.py:23
  222.5 79.4 %collective-permute-start.2 = (bf16[1,1,40,4096]{3,2,1,0:T(8,128)(2,1)S(1)}, bf16[1,1,40,4096]{3,2,1,0:T(8,128)(2,1)}, u32[]{:S(2)}, u32[]{:S(2)}) collective-permute-start(bf16[1,1,40,4096]{3,2,1,0:T(8,128)(2,1)S(1)} %copy-done.3), channel_id=1, source_target_pairs={{0,8},{2,10},{4,12},{6,14},{8,0},{10,2},{12,4},{14,6},{1,9},{3,11}... | collective-permute-start | bytes 983048 | tf_op jit(solution)/shard_map/ppermute | solution.py:23
  236.5 67.8 %collective-permute-start.1 = (bf16[1,1,40,4096]{3,2,1,0:T(8,128)(2,1)S(1)}, bf16[1,1,40,4096]{3,2,1,0:T(8,128)(2,1)}, u32[]{:S(2)}, u32[]{:S(2)}) collective-permute-start(bf16[1,1,40,4096]{3,2,1,0:T(8,128)(2,1)S(1)} %copy-done.2), channel_id=1, source_target_pairs={{0,8},{2,10},{4,12},{6,14},{8,0},{10,2},{12,4},{14,6},{1,9},{3,11}... | collective-permute-start | bytes 983048 | tf_op jit(solution)/shard_map/ppermute | solution.py:23
  250.6 19.7 %copy-start.5 = (bf16[1,1,40,4096]{3,2,1,0:T(8,128)(2,1)}, bf16[1,1,40,4096]{3,2,1,0:T(8,128)(2,1)S(1)}, u32[]{:S(2)}) copy-start(bf16[1,1,40,4096]{3,2,1,0:T(8,128)(2,1)S(1)} %collective-permute-done.5.data_ref) | copy-start | bytes 983044
  250.6 56.2 %collective-permute-start = (bf16[1,1,40,4096]{3,2,1,0:T(8,128)(2,1)}, bf16[1,1,40,4096]{3,2,1,0:T(8,128)(2,1)}, u32[]{:S(2)}, u32[]{:S(2)}) collective-permute-start(bf16[1,1,40,4096]{3,2,1,0:T(8,128)(2,1)} %shard_map.96), channel_id=1, source_target_pairs={{0,8},{2,10},{4,12},{6,14},{8,0},{10,2},{12,4},{14,6},{1,9},{3,11}... | collective-permute-start | bytes 983048 | tf_op jit(solution)/shard_map/ppermute | solution.py:23
  309.2 0.6 copy-start.7
